TPU v7x, 32 devices: a whole 2x2x4 slice. The times are simulated.
32 devices in a mesh: dp: 32 (over z, y, x, core), tensor: 1.
Axes of the slice: x: 2, y: 2, z: 4, core: 2. Of those that a mesh axis runs over, the one named last changes fastest.
Arguments:
- latent_raw: bfloat16 [6144, 512], P('dp'), may hold values from -6 to 6
- norm_gain: float32 [512], replicated, may hold values from 0.5 to 1.5
- up_weight: bfloat16 [512, 4096], P(None, 'tensor'), may hold values from -0.25 to 0.25
- grad_kv: bfloat16 [6144, 4096], P('dp', 'tensor'), may hold values from -3 to 3
Outputs:
- latent_grad: bfloat16 [6144, 512], P('dp')
- gain_grad: float32 [512], replicated
- weight_grad: float32 [512, 4096], P('dp', 'tensor')
All inputs are finite; a program needn't handle non-finite values.
Results may differ from a plain program's by a relative error of at most 0.0029.
Values may be sent and summed in bfloat16 or wider, within the bound.
No kernel may reach another device: no remote copies, remote signals or barrier semaphores. Data moves between devices by JAX's collectives and lax.ppermute only.
A program may use at most 64 MiB of HBM per device.

v0:
```python
import jax
import jax.numpy as jnp
from jax import lax
from jax.sharding import PartitionSpec as P

epsilon = 1e-06


def normalize(latent_raw):
    latent_full = latent_raw.astype(jnp.float32)
    inverse = lax.rsqrt(jnp.mean(latent_full * latent_full, axis=-1, keepdims=True) + epsilon)
    return (latent_full * inverse, inverse)


def norm_backward(grad_norm, scaled_rows, inverse, norm_gain):
    upstream = grad_norm * norm_gain
    centred = upstream - scaled_rows * jnp.mean(upstream * scaled_rows, axis=-1, keepdims=True)
    return (inverse * centred).astype(jnp.bfloat16)


def per_device(latent_raw, norm_gain, up_weight, grad_kv):
    scaled_rows, inverse = normalize(latent_raw)
    normed = (scaled_rows * norm_gain).astype(jnp.bfloat16)
    factor = float(latent_raw.shape[0] * lax.axis_size("dp")) ** (-0.5)
    partial_norm = lax.dot_general(
        grad_kv, up_weight, (((1,), (1,)), ((), ())), preferred_element_type=jnp.float32
    )
    grad_norm = lax.psum_scatter(partial_norm, "tensor", scatter_dimension=0, tiled=True)
    row_count = grad_norm.shape[0]
    offset = lax.axis_index("tensor") * row_count
    scaled_part = lax.dynamic_slice_in_dim(scaled_rows, offset, row_count, 0)
    inverse_part = lax.dynamic_slice_in_dim(inverse, offset, row_count, 0)
    gain_local = jnp.sum(grad_norm * scaled_part, axis=0)
    latent_part = norm_backward(grad_norm, scaled_part, inverse_part, norm_gain)
    latent_grad = lax.all_gather(latent_part, "tensor", axis=0, tiled=True)
    gain_grad = lax.psum(gain_local, ("dp", "tensor")) * factor
    weight_partial = lax.dot_general(
        normed, grad_kv, (((0,), (0,)), ((), ())), preferred_element_type=jnp.float32
    )
    weight_grad = lax.psum_scatter(weight_partial, "dp", scatter_dimension=0, tiled=True) * factor
    return (latent_grad, gain_grad, weight_grad)


def solution(mesh):
    in_specs = (P("dp", None), P(), P(None, "tensor"), P("dp", "tensor"))
    out_specs = (P("dp", None), P(), P("dp", "tensor"))
    return jax.shard_map(
        per_device, mesh=mesh, in_specs=in_specs, out_specs=out_specs, check_vma=False
    )
```

profile of v0, /device:TPU:0, one launch (start us, length us, event | category | flops | bytes accessed | tf_op | source)
XLA Modules:
  0.0 175.9 jit_solution(13392894614203619147)
XLA Ops:
  7.2 0.0 copy-start
  7.2 0.0 reduce-scatter.2.cloned.1.call-start
  7.2 1.2 fusion.10
  8.4 0.3 copy-done
  8.7 5.5 %fusion.11 = f32[512,4096]{1,0:T(8,128)} fusion(bf16[192,4096]{1,0:T(8,128)(2,1)S(1)} %copy-done, bf16[192,512]{1,0:T(8,128)(2,1)} %param.4, f32[512]{0:T(512)} %param.5, f32[192]{0:T(256)S(1)} %add_rsqrt_fusion), kind=kOutput, calls=%fused_computation.13 | convolution fusion | flops 805699584 | bytes 10160896 | tf_op jit(solution)/shard_map/dot_general | solution.py:37
  14.2 0.0 copy-start.1
  14.2 0.0 copy-start.2
  14.2 0.0 reduce-scatter.2.cloned.1.call-update
  14.2 0.9 copy-done.1
  15.1 0.0 copy-done.2
  15.1 3.8 %fusion.8 = (f32[512]{0:T(512)S(1)}, f32[192]{0:T(256)S(1)}, f32[192,512]{1,0:T(8,128)S(1)}) fusion(bf16[192,512]{1,0:T(8,128)(2,1)S(1)} %copy-done.1, f32[192]{0:T(256)S(1)} %add_rsqrt_fusion, f32[512]{0:T(512)S(1)} %copy-done.2, bf16[192,4096]{1,0:T(8,128)(2,1)S(1)} %copy-done, bf16[512,4096]{1,0:T(8,128)(2,1)} %param.6), kind=kOutput, calls=%fused_computation.10 | convolution fusion | flops 805993792 | bytes 6362624 | tf_op jit(solution)/shard_map/dot_general | solution.py:25
  19.0 44.0 %psum.7 = f32[512]{0:T(512)S(1)} all-reduce(f32[512]{0:T(512)S(1)} %get-tuple-element.3), channel_id=1, replica_groups=mesh['dp'=32,'tensor'=1] {'dp','tensor'}, use_global_device_ids=true, to_apply=%region_3.0 | all-reduce | flops 512 | bytes 4096 | tf_op jit(solution)/shard_map/psum | solution.py:36
  63.0 0.6 broadcast_multiply_fusion.1
  63.6 0.9 fusion.7
  64.4 103.0 %reduce-scatter.2.cloned.1.call-done = f32[16,4096]{1,0:T(8,128)} async-done(((f32[512,4096]{1,0:T(8,128)}), f32[16,4096]{1,0:T(8,128)}) %reduce-scatter.2.cloned.1.call-update) | async-done | bytes 262160 | tf_op jit(solution)/shard_map/reduce_scatter | solution.py:40
  167.4 1.7 broadcast_multiply_fusion
  (2 shorter events, 0.0 us)
Async XLA Ops:
  7.2 1.5 copy-start
  7.2 160.2 %reduce-scatter.2.cloned.1.call-start = ((), (), s32[]{:S(2)}) async-start(), calls=%async_computation.1 | async-start | bytes 8650752 | tf_op jit(solution)/shard_map/reduce_scatter | solution.py:40
  14.2 0.9 copy-start.1
  14.2 0.9 copy-start.2
Sparse Core Ops, SparseCore 0:
  14.3 153.0 reduce-scatter.1
where the time goes:
time: 176 us
  waiting for transfers between devices  103 us (59%)
  blocking collectives  44 us (25%)
  between operations  14.1 us (8%)
  matrix products  9.36 us (5%)
  other arithmetic  4.27 us (2%)
    reduce_scatter x1, waiting for transfers between devices, per_device(): lax.psum_scatter(weight_partial, 'dp', scatter_dimension=0, tiled=True)  103 us
    psum x1, blocking collectives, per_device(): gain_grad = lax.psum(gain_local, ('dp', 'tensor')) * factor  44 us
    dot_general x1, matrix products, per_device(): lax.dot_general(normed, grad_kv, (((0,), (0,)), ((), ())), preferred_elem...  5.52 us
    dot_general x1, matrix products, per_device(): lax.dot_general(grad_kv, up_weight, (((1,), (1,)), ((), ())), preferred_e...  3.83 us
  transfers between devices with their start and end apart: 1, of which 1 were waited for; matrix products, arithmetic and copies ran while one was open for 3% of the time, Pallas kernels for 0%

commit v1 on v0

--- a/solution.py
+++ b/solution.py
@@ -33,7 +33,7 @@
     gain_local = jnp.sum(grad_norm * scaled_part, axis=0)
     latent_part = norm_backward(grad_norm, scaled_part, inverse_part, norm_gain)
     latent_grad = lax.all_gather(latent_part, "tensor", axis=0, tiled=True)
-    gain_grad = lax.psum(gain_local, ("dp", "tensor")) * factor
+    gain_grad = jnp.sum(lax.all_gather(gain_local, ("dp", "tensor")), axis=0) * factor
     weight_partial = lax.dot_general(
         normed, grad_kv, (((0,), (0,)), ((), ())), preferred_element_type=jnp.float32
     )

time: 176 us -> 176 us (level)
    psum x1 -> x0, blocking collectives: 44 us -> none  [per_device(): gain_grad = lax.psum(gain_local, ('dp', 'tensor')) * factor]
    all_gather x0 -> x1, blocking collectives: none -> 43.6 us  [per_device(): lax.all_gather(gain_local, ('dp', 'tensor'))]
where the time goes in v1:
time: 176 us
  waiting for transfers between devices  103 us (59%)
  blocking collectives  43.6 us (25%)
  between operations  14.1 us (8%)
  matrix products  9.36 us (5%)
  other arithmetic  4.34 us (2%)
    reduce_scatter x1, waiting for transfers between devices, per_device(): lax.psum_scatter(weight_partial, 'dp', scatter_dimension=0, tiled=True)  103 us
    all_gather x1, blocking collectives, per_device(): lax.all_gather(gain_local, ('dp', 'tensor'))  43.6 us
    dot_general x1, matrix products, per_device(): lax.dot_general(normed, grad_kv, (((0,), (0,)), ((), ())), preferred_elem...  5.52 us
    dot_general x1, matrix products, per_device(): lax.dot_general(grad_kv, up_weight, (((1,), (1,)), ((), ())), preferred_e...  3.83 us
  transfers between devices with their start and end apart: 1, of which 1 were waited for; matrix products, arithmetic and copies ran while one was open for 3% of the time, Pallas kernels for 0%

profile of v1, /device:TPU:0, one launch (start us, length us, event | category | flops | bytes accessed | tf_op | source)
XLA Modules:
  0.0 175.9 jit_solution(3146325256524454540)
XLA Ops:
  7.2 0.0 copy-start
  7.2 0.0 reduce-scatter.2.cloned.1.call-start
  7.2 1.2 fusion.10
  8.4 0.3 copy-done
  8.7 5.5 %fusion.11 = f32[512,4096]{1,0:T(8,128)} fusion(bf16[192,4096]{1,0:T(8,128)(2,1)S(1)} %copy-done, bf16[192,512]{1,0:T(8,128)(2,1)} %param.4, f32[512]{0:T(512)} %param.5, f32[192]{0:T(256)S(1)} %add_rsqrt_fusion), kind=kOutput, calls=%fused_computation.13 | convolution fusion | flops 805699584 | bytes 10160896 | tf_op jit(solution)/shard_map/dot_general | solution.py:37
  14.2 0.0 copy-start.1
  14.2 0.0 copy-start.2
  14.2 0.0 reduce-scatter.2.cloned.1.call-update
  14.2 0.9 copy-done.1
  15.1 0.0 copy-done.2
  15.1 3.8 %fusion.8 = (f32[512]{0:T(512)S(1)}, f32[192]{0:T(256)S(1)}, f32[192,512]{1,0:T(8,128)S(1)}) fusion(bf16[192,512]{1,0:T(8,128)(2,1)S(1)} %copy-done.1, f32[192]{0:T(256)S(1)} %add_rsqrt_fusion, f32[512]{0:T(512)S(1)} %copy-done.2, bf16[192,4096]{1,0:T(8,128)(2,1)S(1)} %copy-done, bf16[512,4096]{1,0:T(8,128)(2,1)} %param.6), kind=kOutput, calls=%fused_computation.10 | convolution fusion | flops 805993792 | bytes 6362624 | tf_op jit(solution)/shard_map/dot_general | solution.py:25
  19.0 43.6 %all-gather.1 = f32[32,1,512]{2,1,0:T(1,128)S(1)} all-gather(f32[1,1,512]{2,1,0:T(1,128)S(1)} %bitcast.4), channel_id=2, replica_groups=mesh['dp'=32,'tensor'=1] {'dp','tensor'}, dimensions={0}, use_global_device_ids=true | all-gather | bytes 67584 | tf_op jit(solution)/shard_map/all_gather | solution.py:36
  62.6 0.1 reduce_sum.39
  62.6 0.6 broadcast_multiply_fusion.1
  63.2 0.9 fusion.7
  64.1 103.3 %reduce-scatter.2.cloned.1.call-done = f32[16,4096]{1,0:T(8,128)} async-done(((f32[512,4096]{1,0:T(8,128)}), f32[16,4096]{1,0:T(8,128)}) %reduce-scatter.2.cloned.1.call-update) | async-done | bytes 262160 | tf_op jit(solution)/shard_map/reduce_scatter | solution.py:40
  167.3 1.7 broadcast_multiply_fusion
  (2 shorter events, 0.0 us)
Async XLA Ops:
  7.2 1.5 copy-start
  7.2 160.2 %reduce-scatter.2.cloned.1.call-start = ((), (), s32[]{:S(2)}) async-start(), calls=%async_computation.1 | async-start | bytes 8650752 | tf_op jit(solution)/shard_map/reduce_scatter | solution.py:40
  14.2 0.9 copy-start.1
  14.2 0.9 copy-start.2
Sparse Core Ops, SparseCore 0:
  14.3 152.9 reduce-scatter.1
